TPU v7x, 256 devices: a whole 4x4x8 slice. The times are simulated.
256 devices in a mesh: ctx: 32 (over x, z), pb: 2 (over core), ga: 4 (over y).
Axes of the slice: x: 4, y: 4, z: 8, core: 2. Of those that a mesh axis runs over, the one named last changes fastest.
Arguments:
- queries: bfloat16 [8192, 12288], P(('ctx', 'pb'), 'ga'), may hold values from -128 to 128
- stretch_keys: bfloat16 [8192, 768], P(('ctx', 'pb'), 'ga'), may hold values from -16 to 16
- stretch_values: bfloat16 [8192, 512], P(('ctx', 'pb'), 'ga'), may hold values from -6 to 6
- prior_cache_keys: bfloat16 [131072, 768], P('ctx', 'ga'), may hold values from -16 to 16
- cache_values: bfloat16 [131072, 512], P('ctx', 'ga'), may hold values from -6 to 6
- block_lengths: int32 [32, 256], P('ctx'), may hold values from 1 to 32, 4096 in all within a row
- compress_weights: float32 [4, 32], P('ga'), may hold values from 0.1 to 1.9
- selections: int32 [128, 4, 13], P(('ctx', 'pb'), 'ga'), may hold values from 1 to 2045, as said below
- gate_logits: float32 [3, 8192, 64], P(None, ('ctx', 'pb'), 'ga'), may hold values from -6 to 6
Outputs:
- attended: bfloat16 [8192, 8192], P(('ctx', 'pb'), 'ga')
Inputs may be any that keep to these rules, and one draw needn't show every extreme that they name: `block_lengths`: each row belongs to one cache shard and sums to 4096; its largest entry is 32. `selections`: each row lists 13 different blocks, never the first or one of the last two blocks of a cache shard (a shard holds 64 blocks). Over the 2 rows of one device and one group at most 2 listed blocks lie in one cache shard, and for each group one cache shard holds exactly 2 of every device's listed blocks.
All inputs are finite; a program needn't handle non-finite values.
Results may differ from a plain program's by a relative error of at most 0.011.
Values may be sent and summed in bfloat16 or wider, within the bound.
A program may use at most 128 MiB of HBM per device.

v0:
```python
import math
import jax
import jax.numpy as jnp
from jax import lax
from jax.sharding import PartitionSpec as P

SBLK = 64
WINDOW = 512
floor_score = -1e30


def passed_along(value, axis, steps):
    count = lax.axis_size(axis)
    first, last = (max(0, -steps), min(count, count - steps))
    return lax.ppermute(value, axis, [(source, source + steps) for source in range(first, last)])


def compress_rows(cache_rows, value_rows, lengths, branch_weights):
    span = cache_rows.shape[0]
    starts = jnp.cumsum(lengths) - lengths
    positions = jnp.arange(span, dtype=jnp.int32)
    group_member = (positions[None, :] >= starts[:, None]) & (
        positions[None, :] < (starts + lengths)[:, None]
    )
    offsets = jnp.sum(jnp.where(group_member, positions[None, :] - starts[:, None], 0), axis=0)
    lookup = jnp.arange(branch_weights.shape[0], dtype=jnp.int32)
    token_weight = jnp.sum(
        jnp.where(offsets[:, None] == lookup[None, :], branch_weights[None, :], 0.0), axis=1
    )
    spread = 1.0 / jnp.sqrt(lengths.astype(jnp.float32))
    matrix = jnp.where(group_member, token_weight[None, :] * spread[:, None], 0.0).astype(
        jnp.bfloat16
    )
    packed_keys = jnp.dot(matrix, cache_rows, preferred_element_type=jnp.float32).astype(
        jnp.bfloat16
    )
    packed_values = jnp.dot(matrix, value_rows, preferred_element_type=jnp.float32).astype(
        jnp.bfloat16
    )
    return (packed_keys, packed_values)


def wanted_blocks(listed_ids, block_total):
    flat_ids = listed_ids.reshape(-1)
    always_on = jnp.array([0, block_total - 2, block_total - 1], dtype=jnp.int32)
    flat_ids = jnp.concatenate([always_on, flat_ids])
    return flat_ids


def slot_table(flat_ids, per_shard, slot_width):
    owners = flat_ids // per_shard
    position = jnp.arange(flat_ids.shape[0], dtype=jnp.int32)
    before = (owners[None, :] == owners[:, None]) & (position[None, :] < position[:, None])
    rank_count = jnp.sum(before.astype(jnp.int32), axis=1)
    return (owners * slot_width + rank_count, flat_ids % per_shard)


def asked_table(slots, offsets, shards, slot_width):
    places = jnp.arange(shards * slot_width, dtype=jnp.int32)
    matches = slots[:, None] == places[None, :]
    full_table = jnp.sum(jnp.where(matches, offsets[:, None], 0), axis=0)
    return full_table.reshape(shards, slot_width)


def on_device(
    queries,
    stretch_keys,
    stretch_values,
    prior_cache_keys,
    cache_values,
    block_lengths,
    compress_weights,
    selections,
    gate_logits,
):
    query_count = queries.shape[0]
    head_count = gate_logits.shape[2]
    key_width = prior_cache_keys.shape[1]
    value_width = cache_values.shape[1]
    score_scale = 1.0 / math.sqrt(key_width)
    query_rows = queries.reshape(query_count * head_count, key_width)
    row_count = query_rows.shape[0]
    shards = lax.axis_size("ctx")
    packed_keys, packed_values = compress_rows(
        prior_cache_keys, cache_values, block_lengths[0], compress_weights[0]
    )
    start_state = (
        jnp.full((row_count,), floor_score, jnp.float32),
        jnp.zeros((row_count,), jnp.float32),
        jnp.zeros((row_count, value_width), jnp.float32),
    )
    piece_keys = lax.all_gather(packed_keys, "ctx", axis=0, tiled=True)
    piece_values = lax.all_gather(packed_values, "ctx", axis=0, tiled=True)
    length = piece_keys.shape[0]
    stride = math.gcd(length, 1024)
    key_block = piece_keys.reshape(length // stride, stride, key_width)
    value_block = piece_values.reshape(length // stride, stride, value_width)

    def absorb(carry_state, operand):
        row_peak, running_total, blended = carry_state
        some_keys, some_values = operand
        scores = (
            lax.dot_general(
                query_rows, some_keys, (((1,), (1,)), ((), ())), preferred_element_type=jnp.float32
            )
            * score_scale
        )
        new_peak = jnp.maximum(row_peak, jnp.max(scores, axis=1))
        factor = jnp.exp(row_peak - new_peak)
        branch_weights = jnp.exp(scores - new_peak[:, None])
        running_total = running_total * factor + jnp.sum(branch_weights, axis=1)
        blended = blended * factor[:, None] + jnp.dot(
            branch_weights.astype(jnp.bfloat16), some_values, preferred_element_type=jnp.float32
        )
        return ((new_peak, running_total, blended), None)

    row_peak, running_total, blended = lax.scan(absorb, start_state, (key_block, value_block))[0]
    compressed_out = (blended / running_total[:, None]).reshape(
        query_count, head_count, value_width
    )
    listed_ids = selections[:, 0, :]
    query_blocks, listed = listed_ids.shape
    per_shard = prior_cache_keys.shape[0] // SBLK
    block_total = per_shard * shards
    slot_bound = max(2, (query_blocks * listed + shards - 1) // shards)
    key_blocks = prior_cache_keys.reshape(per_shard, SBLK, key_width)
    value_blocks = cache_values.reshape(per_shard, SBLK, value_width)
    slot_width = slot_bound + 2
    slots, offsets = slot_table(wanted_blocks(listed_ids, block_total), per_shard, slot_width)
    asked_here = asked_table(slots, offsets, shards, slot_width)
    asked_for = lax.all_to_all(asked_here, "ctx", split_axis=0, concat_axis=0, tiled=True)
    item_count = asked_for.shape[1]
    flat_asked = asked_for.reshape(-1)
    sent_keys = jnp.take(key_blocks, flat_asked, axis=0).reshape(
        shards, item_count, SBLK, key_width
    )
    sent_values = jnp.take(value_blocks, flat_asked, axis=0).reshape(
        shards, item_count, SBLK, value_width
    )
    got_keys = lax.all_to_all(sent_keys, "ctx", split_axis=0, concat_axis=0, tiled=True)
    got_values = lax.all_to_all(sent_values, "ctx", split_axis=0, concat_axis=0, tiled=True)
    picked_keys = jnp.take(got_keys.reshape(shards * slot_width, SBLK, key_width), slots, axis=0)
    picked_values = jnp.take(
        got_values.reshape(shards * slot_width, SBLK, value_width), slots, axis=0
    )
    fixed_keys = picked_keys[:3]
    fixed_values = picked_values[:3]
    listed_keys = picked_keys[3:]
    listed_values = picked_values[3:]
    selected_keys = jnp.concatenate(
        [
            jnp.broadcast_to(fixed_keys[None], (query_blocks, 3, SBLK, key_width)),
            listed_keys.reshape(query_blocks, listed, SBLK, key_width),
        ],
        axis=1,
    ).reshape(query_blocks, (3 + listed) * SBLK, key_width)
    chosen_values = jnp.concatenate(
        [
            jnp.broadcast_to(fixed_values[None], (query_blocks, 3, SBLK, value_width)),
            listed_values.reshape(query_blocks, listed, SBLK, value_width),
        ],
        axis=1,
    ).reshape(query_blocks, (3 + listed) * SBLK, value_width)
    grouped_rows = queries.reshape(query_blocks, query_count // query_blocks, head_count, key_width)
    scores = (
        jnp.einsum(
            "rjve,rse->rjvs", grouped_rows, selected_keys, preferred_element_type=jnp.float32
        )
        * score_scale
    )
    row_peak = jnp.max(scores, axis=3, keepdims=True)
    branch_weights = jnp.exp(scores - row_peak)
    row_total = jnp.sum(branch_weights, axis=3, keepdims=True)
    selected_out = (
        jnp.einsum(
            "bqhk,bkv->bqhv",
            branch_weights.astype(jnp.bfloat16),
            chosen_values,
            preferred_element_type=jnp.float32,
        )
        / row_total
    )
    selected_out = selected_out.reshape(query_count, head_count, value_width)
    reach_count = max(1, WINDOW // query_count)
    earlier_keys = []
    earlier_values = []
    for distance in range(reach_count, 0, -1):
        moved_keys, moved_values = passed_along(
            (stretch_keys, stretch_values), ("ctx", "pb"), distance
        )
        earlier_keys.append(moved_keys)
        earlier_values.append(moved_values)
    window_rows = jnp.concatenate(earlier_keys + [stretch_keys], axis=0)
    window_values = jnp.concatenate(earlier_values + [stretch_values], axis=0)
    first_query = lax.axis_index(("ctx", "pb")) * query_count
    query_pos = first_query + jnp.arange(query_count, dtype=jnp.int32)
    key_pos = (
        first_query - reach_count * query_count + jnp.arange(window_rows.shape[0], dtype=jnp.int32)
    )
    distance_grid = query_pos[:, None] - key_pos[None, :]
    allowed = (distance_grid >= 0) & (distance_grid < WINDOW) & (key_pos[None, :] >= 0)
    near_scores = (
        jnp.einsum(
            "qhd,kd->qhk",
            queries.reshape(query_count, head_count, key_width),
            window_rows,
            preferred_element_type=jnp.float32,
        )
        * score_scale
    )
    near_scores = jnp.where(allowed[:, None, :], near_scores, floor_score)
    near_peak = jnp.max(near_scores, axis=2, keepdims=True)
    near_weights = jnp.exp(near_scores - near_peak)
    near_total = jnp.sum(near_weights, axis=2, keepdims=True)
    windowed_out = (
        jnp.einsum(
            "qhk,kv->qhv",
            near_weights.astype(jnp.bfloat16),
            window_values,
            preferred_element_type=jnp.float32,
        )
        / near_total
    )
    gate_values = jax.nn.sigmoid(gate_logits)
    attended = (
        gate_values[0][..., None] * compressed_out
        + gate_values[1][..., None] * selected_out
        + gate_values[2][..., None] * windowed_out
    )
    return attended.reshape(query_count, head_count * value_width).astype(jnp.bfloat16)


def solution(mesh):
    placed = (
        P(("ctx", "pb"), "ga"),
        P(("ctx", "pb"), "ga"),
        P(("ctx", "pb"), "ga"),
        P("ctx", "ga"),
        P("ctx", "ga"),
        P("ctx", None),
        P("ga", None),
        P(("ctx", "pb"), "ga", None),
        P(None, ("ctx", "pb"), "ga"),
    )
    return jax.shard_map(
        on_device, mesh=mesh, in_specs=placed, out_specs=P(("ctx", "pb"), "ga"), check_vma=False
    )
```

profile of v0, /device:TPU:24, one launch (start us, length us, event | category | flops | bytes accessed | tf_op | source)
XLA Modules:
  0.0 363.3 jit_solution(14902906855570495999)
XLA Ops:
  11.5 3.3 fusion.34
  17.9 11.3 %all-to-all-start = ((s32[32,1,4]{2,1,0:T(1,128)}), s32[32,1,4]{2,1,0:T(1,128)S(1)}, u32[]{:S(2)}, u32[]{:S(2)}) async-start(s32[32,1,4]{2,1,0:T(1,128)} %bitcast.9), calls=%async_computation | async-start | bytes 32768 | tf_op jit(solution)/shard_map/all_to_all | solution.py:131
  29.2 4.6 %collective-permute-start = (bf16[128,192]{0,1:T(8,128)(2,1)S(1)}, bf16[128,192]{0,1:T(8,128)(2,1)S(1)}, u32[]{:S(2)}, u32[]{:S(2)}) collective-permute-start(bf16[128,192]{0,1:T(8,128)(2,1)S(1)} %copy-done.8), channel_id=1, source_target_pairs={{0,16},{4,20},{8,24},{12,28},{16,32},{20,36},{24,40},{28,44},{32,4... | collective-permute-start | bytes 147464 | tf_op jit(solution)/shard_map/ppermute | solution.py:15
  35.8 4.6 %collective-permute-start.2 = (bf16[128,192]{0,1:T(8,128)(2,1)S(1)}, bf16[128,192]{0,1:T(8,128)(2,1)S(1)}, u32[]{:S(2)}, u32[]{:S(2)}) collective-permute-start(bf16[128,192]{0,1:T(8,128)(2,1)S(1)} %copy-done.8), channel_id=1, source_target_pairs={{0,8},{4,12},{8,16},{12,20},{16,24},{20,28},{24,32},{28,36},{32,40... | collective-permute-start | bytes 147464 | tf_op jit(solution)/shard_map/ppermute | solution.py:15
  40.4 3.1 collective-permute-start.3
  49.8 9.3 %all-to-all-start.2 = ((bf16[32,4,64,128]{3,2,1,0:T(8,128)(2,1)}), bf16[32,4,64,128]{3,2,1,0:T(8,128)(2,1)}, u32[]{:S(2)}, u32[]{:S(2)}) async-start(bf16[32,4,64,128]{3,2,1,0:T(8,128)(2,1)} %broadcast_select_fusion.1), calls=%async_computation.2 | async-start | bytes 4194304 | tf_op jit(solution)/shard_map/all_to_all | solution.py:141
  61.2 3.9 %copy.85 = bf16[4096,192]{1,0:T(8,128)(2,1)} copy(bf16[4096,192]{0,1:T(8,128)(2,1)} %param.15) | data formatting | bytes 3145728 | tf_op args[3]
  70.6 4.5 %gather_fusion = bf16[128,64,192]{2,1,0:T(8,128)(2,1)} fusion(bf16[64,64,192]{2,1,0:T(8,128)(2,1)} %bitcast.102, s32[1024]{0:T(1024)} %copy-done.15), kind=kCustom, calls=%fused_computation | custom fusion | bytes 6291968 | tf_op jit(solution)/shard_map/jit(_take)/gather | solution.py:134
  75.1 4.6 %broadcast_select_fusion = bf16[32,4,64,192]{3,2,1,0:T(8,128)(2,1)} fusion(bf16[32,4,64,192]{3,2,1,0:T(8,128)(2,1)} %bitcast.103, pred[32,4]{1,0:T(8,128)(4,1)S(1)} %copy.84), kind=kLoop, calls=%fused_computation.42 | loop fusion | flops 1572864 | bytes 6291584 | tf_op jit(solution)/shard_map/jit(_take)/select_n | solution.py:134
  82.3 30.3 %collective-permute-done.5 = bf16[128,128]{0,1:T(8,128)(2,1)S(1)} collective-permute-done((bf16[128,128]{0,1:T(8,128)(2,1)S(1)}, bf16[128,128]{0,1:T(8,128)(2,1)S(1)}, u32[]{:S(2)}, u32[]{:S(2)}) %collective-permute-start.5) | collective-permute-done | bytes 32800 | tf_op jit(solution)/shard_map/ppermute | solution.py:15
  112.5 6.4 %collective-permute-start.6 = (bf16[128,128]{0,1:T(8,128)(2,1)S(1)}, bf16[128,128]{0,1:T(8,128)(2,1)S(1)}, u32[]{:S(2)}, u32[]{:S(2)}) collective-permute-start(bf16[128,128]{0,1:T(8,128)(2,1)S(1)} %copy.92), channel_id=1, source_target_pairs={{0,8},{4,12},{8,16},{12,20},{16,24},{20,28},{24,32},{28,36},{32,40... | collective-permute-start | bytes 98312 | tf_op jit(solution)/shard_map/ppermute | solution.py:15
  128.1 17.3 %all-to-all-start.1 = ((bf16[32,4,64,192]{3,2,1,0:T(8,128)(2,1)}), bf16[32,4,64,192]{3,2,1,0:T(8,128)(2,1)}, u32[]{:S(2)}, u32[]{:S(2)}) async-start(bf16[32,4,64,192]{3,2,1,0:T(8,128)(2,1)} %broadcast_select_fusion), calls=%async_computation.1 | async-start | bytes 8388608 | tf_op jit(solution)/shard_map/all_to_all | solution.py:140
  148.7 6.0 %copy.102 = bf16[8192,192]{1,0:T(8,128)(2,1)} copy(bf16[8192,192]{0,1:T(8,128)(2,1)} %all-gather.3.cloned.1.call-done) | data formatting | bytes 6291456
  154.6 69.5 %all-gather.5.cloned.1.call-done = bf16[8192,128]{1,0:T(8,128)(2,1)} async-done(((bf16[256,128]{1,0:T(8,128)(2,1)}), bf16[8192,128]{1,0:T(8,128)(2,1)}) %all-gather.5.cloned.1.call-update) | async-done | bytes 2097168 | tf_op jit(solution)/shard_map/all_gather | solution.py:93
  224.1 114.3 %while.15 = (s32[]{:T(128)}, f32[2048]{0:T(1024)S(1)}, f32[2048]{0:T(1024)S(1)}, f32[2048,128]{1,0:T(8,128)S(1)}, bf16[8,1024,192]{2,1,0:T(8,128)(2,1)}, /*index...) while((s32[]{:T(128)}, f32[2048]{0:T(1024)S(1)}, ...), condition=%wide.region_7.8_spmd.clone, body=%wide.region_4.7_spmd.clone.sunk | while | flops 1359751168 | bytes 62522500 | solution.py:117
  224.1 5.5 %multiply_reduce_fusion.2 = (f32[2048]{0:T(1024)S(1)}, f32[1024,2048]{1,0:T(8,128)}) fusion(bf16[2048,192]{1,0:T(8,128)(2,1)S(1)} %get-tuple-element.209, bf16[8,1024,192]{2,1,0:T(8,128)(2,1)} %get-tuple-element.208, s32[]{:T(128)} %get-tuple-element.195), kind=kOutput, calls=%fused_computation.5.clone.1 | convolution fusion | flops 809498624 | bytes 9708032 | tf_op jit(solution)/shard_map/while/body/eval_jaxpr/dot_general | solution.py:103
  229.7 4.9 %fusion.72 = f32[2048]{0:T(1024)S(1)} fusion(f32[1024,2048]{1,0:T(8,128)} %get-tuple-element.183, f32[2048]{0:T(1024)S(1)} %select_maximum_fusion.2), kind=kLoop, calls=%fused_computation.7.clone.1 | loop fusion | flops 6289408 | bytes 8404992 | tf_op jit(solution)/shard_map/while/body/eval_jaxpr/reduce_sum | solution.py:111
  238.4 5.6 %multiply_reduce_fusion.2 = (f32[2048]{0:T(1024)S(1)}, f32[1024,2048]{1,0:T(8,128)}) fusion(bf16[2048,192]{1,0:T(8,128)(2,1)S(1)} %get-tuple-element.209, bf16[8,1024,192]{2,1,0:T(8,128)(2,1)} %get-tuple-element.208, s32[]{:T(128)} %get-tuple-element.195), kind=kOutput, calls=%fused_computation.5.clone.1 | convolution fusion | flops 809498624 | bytes 9708032 | tf_op jit(solution)/shard_map/while/body/eval_jaxpr/dot_general | solution.py:103
  244.0 4.9 %fusion.72 = f32[2048]{0:T(1024)S(1)} fusion(f32[1024,2048]{1,0:T(8,128)} %get-tuple-element.183, f32[2048]{0:T(1024)S(1)} %select_maximum_fusion.2), kind=kLoop, calls=%fused_computation.7.clone.1 | loop fusion | flops 6289408 | bytes 8404992 | tf_op jit(solution)/shard_map/while/body/eval_jaxpr/reduce_sum | solution.py:111
  252.7 5.6 %multiply_reduce_fusion.2 = (f32[2048]{0:T(1024)S(1)}, f32[1024,2048]{1,0:T(8,128)}) fusion(bf16[2048,192]{1,0:T(8,128)(2,1)S(1)} %get-tuple-element.209, bf16[8,1024,192]{2,1,0:T(8,128)(2,1)} %get-tuple-element.208, s32[]{:T(128)} %get-tuple-element.195), kind=kOutput, calls=%fused_computation.5.clone.1 | convolution fusion | flops 809498624 | bytes 9708032 | tf_op jit(solution)/shard_map/while/body/eval_jaxpr/dot_general | solution.py:103
  258.3 4.9 %fusion.72 = f32[2048]{0:T(1024)S(1)} fusion(f32[1024,2048]{1,0:T(8,128)} %get-tuple-element.183, f32[2048]{0:T(1024)S(1)} %select_maximum_fusion.2), kind=kLoop, calls=%fused_computation.7.clone.1 | loop fusion | flops 6289408 | bytes 8404992 | tf_op jit(solution)/shard_map/while/body/eval_jaxpr/reduce_sum | solution.py:111
  267.0 5.6 %multiply_reduce_fusion.2 = (f32[2048]{0:T(1024)S(1)}, f32[1024,2048]{1,0:T(8,128)}) fusion(bf16[2048,192]{1,0:T(8,128)(2,1)S(1)} %get-tuple-element.209, bf16[8,1024,192]{2,1,0:T(8,128)(2,1)} %get-tuple-element.208, s32[]{:T(128)} %get-tuple-element.195), kind=kOutput, calls=%fused_computation.5.clone.1 | convolution fusion | flops 809498624 | bytes 9708032 | tf_op jit(solution)/shard_map/while/body/eval_jaxpr/dot_general | solution.py:103
  272.6 4.9 %fusion.72 = f32[2048]{0:T(1024)S(1)} fusion(f32[1024,2048]{1,0:T(8,128)} %get-tuple-element.183, f32[2048]{0:T(1024)S(1)} %select_maximum_fusion.2), kind=kLoop, calls=%fused_computation.7.clone.1 | loop fusion | flops 6289408 | bytes 8404992 | tf_op jit(solution)/shard_map/while/body/eval_jaxpr/reduce_sum | solution.py:111
  281.3 5.6 %multiply_reduce_fusion.2 = (f32[2048]{0:T(1024)S(1)}, f32[1024,2048]{1,0:T(8,128)}) fusion(bf16[2048,192]{1,0:T(8,128)(2,1)S(1)} %get-tuple-element.209, bf16[8,1024,192]{2,1,0:T(8,128)(2,1)} %get-tuple-element.208, s32[]{:T(128)} %get-tuple-element.195), kind=kOutput, calls=%fused_computation.5.clone.1 | convolution fusion | flops 809498624 | bytes 9708032 | tf_op jit(solution)/shard_map/while/body/eval_jaxpr/dot_general | solution.py:103
  286.8 4.9 %fusion.72 = f32[2048]{0:T(1024)S(1)} fusion(f32[1024,2048]{1,0:T(8,128)} %get-tuple-element.183, f32[2048]{0:T(1024)S(1)} %select_maximum_fusion.2), kind=kLoop, calls=%fused_computation.7.clone.1 | loop fusion | flops 6289408 | bytes 8404992 | tf_op jit(solution)/shard_map/while/body/eval_jaxpr/reduce_sum | solution.py:111
  295.6 5.6 %multiply_reduce_fusion.2 = (f32[2048]{0:T(1024)S(1)}, f32[1024,2048]{1,0:T(8,128)}) fusion(bf16[2048,192]{1,0:T(8,128)(2,1)S(1)} %get-tuple-element.209, bf16[8,1024,192]{2,1,0:T(8,128)(2,1)} %get-tuple-element.208, s32[]{:T(128)} %get-tuple-element.195), kind=kOutput, calls=%fused_computation.5.clone.1 | convolution fusion | flops 809498624 | bytes 9708032 | tf_op jit(solution)/shard_map/while/body/eval_jaxpr/dot_general | solution.py:103
  301.1 4.9 %fusion.72 = f32[2048]{0:T(1024)S(1)} fusion(f32[1024,2048]{1,0:T(8,128)} %get-tuple-element.183, f32[2048]{0:T(1024)S(1)} %select_maximum_fusion.2), kind=kLoop, calls=%fused_computation.7.clone.1 | loop fusion | flops 6289408 | bytes 8404992 | tf_op jit(solution)/shard_map/while/body/eval_jaxpr/reduce_sum | solution.py:111
  309.9 5.6 %multiply_reduce_fusion.2 = (f32[2048]{0:T(1024)S(1)}, f32[1024,2048]{1,0:T(8,128)}) fusion(bf16[2048,192]{1,0:T(8,128)(2,1)S(1)} %get-tuple-element.209, bf16[8,1024,192]{2,1,0:T(8,128)(2,1)} %get-tuple-element.208, s32[]{:T(128)} %get-tuple-element.195), kind=kOutput, calls=%fused_computation.5.clone.1 | convolution fusion | flops 809498624 | bytes 9708032 | tf_op jit(solution)/shard_map/while/body/eval_jaxpr/dot_general | solution.py:103
  315.4 4.9 %fusion.72 = f32[2048]{0:T(1024)S(1)} fusion(f32[1024,2048]{1,0:T(8,128)} %get-tuple-element.183, f32[2048]{0:T(1024)S(1)} %select_maximum_fusion.2), kind=kLoop, calls=%fused_computation.7.clone.1 | loop fusion | flops 6289408 | bytes 8404992 | tf_op jit(solution)/shard_map/while/body/eval_jaxpr/reduce_sum | solution.py:111
  324.2 5.6 %multiply_reduce_fusion.2 = (f32[2048]{0:T(1024)S(1)}, f32[1024,2048]{1,0:T(8,128)}) fusion(bf16[2048,192]{1,0:T(8,128)(2,1)S(1)} %get-tuple-element.209, bf16[8,1024,192]{2,1,0:T(8,128)(2,1)} %get-tuple-element.208, s32[]{:T(128)} %get-tuple-element.195), kind=kOutput, calls=%fused_computation.5.clone.1 | convolution fusion | flops 809498624 | bytes 9708032 | tf_op jit(solution)/shard_map/while/body/eval_jaxpr/dot_general | solution.py:103
  329.7 4.9 %fusion.72 = f32[2048]{0:T(1024)S(1)} fusion(f32[1024,2048]{1,0:T(8,128)} %get-tuple-element.183, f32[2048]{0:T(1024)S(1)} %select_maximum_fusion.2), kind=kLoop, calls=%fused_computation.7.clone.1 | loop fusion | flops 6289408 | bytes 8404992 | tf_op jit(solution)/shard_map/while/body/eval_jaxpr/reduce_sum | solution.py:111
  349.5 4.9 %add_convert_fusion = bf16[128,16,128]{0,2,1:T(8,128)(2,1)} fusion(f32[128,16,128]{0,2,1:T(8,128)S(1)} %copy.90, f32[128,16,128]{0,2,1:T(8,128)S(1)} %copy.81, f32[640,128,16]{1,0,2:T(8,128)} %copy-done.5, f32[128,16]{0,1:T(8,128)S(1)} %get-tuple-element.133, pred[128,640]{0,1:T(8,128)(4,1)S(1)} %fusion.44, f32[128,16]{0,1:T(8,128)S(1)} %fusion.21, ...), kind=kOutput, calls=%fused_computation.54 | convolution fusion | flops 342622208 | bytes 8151040 | tf_op jit(solution)/shard_map/qhk,kv->qhv/dot_general | solution.py:216
  (180 shorter events, 81.5 us)
Async XLA Ops:
  6.5 40.7 %copy-start = (bf16[4096,128]{1,0:T(8,128)(2,1)S(1)}, bf16[4096,128]{1,0:T(8,128)(2,1)}, u32[]{:S(2)}) copy-start(bf16[4096,128]{1,0:T(8,128)(2,1)} %param.16) | copy-start | bytes 3145732
  6.5 142.1 %all-gather.3.cloned.1.call-start = ((), (), s32[]{:S(2)}) async-start(), calls=%async_computation.3 | async-start | bytes 3244032 | tf_op jit(solution)/shard_map/all_gather | solution.py:92
  11.5 4.0 %copy-start.17 = (s32[2,1,13]{2,1,0:T(1,128)S(1)}, s32[2,1,13]{2,1,0:T(1,128)}, u32[]{:S(2)}) copy-start(s32[2,1,13]{2,1,0:T(1,128)} %param.19) | copy-start | bytes 316
  11.5 4.8 %copy-start.19 = (s32[3]{0:T(128)S(1)}, s32[3]{0:T(128)}, u32[]{:S(2)}) copy-start(s32[3]{0:T(128)} %constant.139.clone) | copy-start | bytes 40
  11.5 17.7 %copy-start.8 = (bf16[128,192]{0,1:T(8,128)(2,1)S(1)}, bf16[128,192]{0,1:T(8,128)(2,1)}, u32[]{:S(2)}) copy-start(bf16[128,192]{0,1:T(8,128)(2,1)} %param.13) | copy-start | bytes 147460
  11.5 32.0 %copy-start.9 = (bf16[128,128]{1,0:T(8,128)(2,1)S(1)}, bf16[128,128]{1,0:T(8,128)(2,1)}, u32[]{:S(2)}) copy-start(bf16[128,128]{1,0:T(8,128)(2,1)} %param.14) | copy-start | bytes 98308
  17.9 28.3 %all-to-all-start = ((s32[32,1,4]{2,1,0:T(1,128)}), s32[32,1,4]{2,1,0:T(1,128)S(1)}, u32[]{:S(2)}, u32[]{:S(2)}) async-start(s32[32,1,4]{2,1,0:T(1,128)} %bitcast.9), calls=%async_computation | async-start | bytes 32768 | tf_op jit(solution)/shard_map/all_to_all | solution.py:131
  29.2 94.3 %collective-permute-start = (bf16[128,192]{0,1:T(8,128)(2,1)S(1)}, bf16[128,192]{0,1:T(8,128)(2,1)S(1)}, u32[]{:S(2)}, u32[]{:S(2)}) collective-permute-start(bf16[128,192]{0,1:T(8,128)(2,1)S(1)} %copy-done.8), channel_id=1, source_target_pairs={{0,16},{4,20},{8,24},{12,28},{16,32},{20,36},{24,40},{28,44},{32,4... | collective-permute-start | bytes 147464 | tf_op jit(solution)/shard_map/ppermute | solution.py:15
  33.8 89.7 %collective-permute-start.1 = (bf16[128,192]{0,1:T(8,128)(2,1)S(1)}, bf16[128,192]{0,1:T(8,128)(2,1)S(1)}, u32[]{:S(2)}, u32[]{:S(2)}) collective-permute-start(bf16[128,192]{0,1:T(8,128)(2,1)S(1)} %copy-done.8), channel_id=1, source_target_pairs={{0,12},{4,16},{8,20},{12,24},{16,28},{20,32},{24,36},{28,40},{32,4... | collective-permute-start | bytes 147464 | tf_op jit(solution)/shard_map/ppermute | solution.py:15
  35.8 87.7 %collective-permute-start.2 = (bf16[128,192]{0,1:T(8,128)(2,1)S(1)}, bf16[128,192]{0,1:T(8,128)(2,1)S(1)}, u32[]{:S(2)}, u32[]{:S(2)}) collective-permute-start(bf16[128,192]{0,1:T(8,128)(2,1)S(1)} %copy-done.8), channel_id=1, source_target_pairs={{0,8},{4,12},{8,16},{12,20},{16,24},{20,28},{24,32},{28,36},{32,40... | collective-permute-start | bytes 147464 | tf_op jit(solution)/shard_map/ppermute | solution.py:15
  40.4 83.2 %collective-permute-start.3 = (bf16[128,192]{0,1:T(8,128)(2,1)S(1)}, bf16[128,192]{0,1:T(8,128)(2,1)S(1)}, u32[]{:S(2)}, u32[]{:S(2)}) collective-permute-start(bf16[128,192]{0,1:T(8,128)(2,1)S(1)} %copy-done.8), channel_id=1, source_target_pairs={{0,4},{4,8},{8,12},{12,16},{16,20},{20,24},{24,28},{28,32},{32,36}... | collective-permute-start | bytes 147464 | tf_op jit(solution)/shard_map/ppermute | solution.py:15
  43.6 36.1 %collective-permute-start.4 = (bf16[128,128]{0,1:T(8,128)(2,1)S(1)}, bf16[128,128]{0,1:T(8,128)(2,1)S(1)}, u32[]{:S(2)}, u32[]{:S(2)}) collective-permute-start(bf16[128,128]{0,1:T(8,128)(2,1)S(1)} %copy.92), channel_id=1, source_target_pairs={{0,16},{4,20},{8,24},{12,28},{16,32},{20,36},{24,40},{28,44},{32,4... | collective-permute-start | bytes 98312 | tf_op jit(solution)/shard_map/ppermute | solution.py:15
  49.8 78.2 %all-to-all-start.2 = ((bf16[32,4,64,128]{3,2,1,0:T(8,128)(2,1)}), bf16[32,4,64,128]{3,2,1,0:T(8,128)(2,1)}, u32[]{:S(2)}, u32[]{:S(2)}) async-start(bf16[32,4,64,128]{3,2,1,0:T(8,128)(2,1)} %broadcast_select_fusion.1), calls=%async_computation.2 | async-start | bytes 4194304 | tf_op jit(solution)/shard_map/all_to_all | solution.py:141
  59.2 5.9 %copy-start.3 = (bf16[128,3072]{1,0:T(8,128)(2,1)S(1)}, bf16[128,3072]{1,0:T(8,128)(2,1)}, u32[]{:S(2)}) copy-start(bf16[128,3072]{1,0:T(8,128)(2,1)} %param.12) | copy-start | bytes 2359300
  59.2 164.9 %all-gather.5.cloned.1.call-start = ((), (), s32[]{:S(2)}) async-start(), calls=%async_computation.4 | async-start | bytes 2162688 | tf_op jit(solution)/shard_map/all_gather | solution.py:93
  61.1 8.5 %copy-start.18 = (s32[3,1]{0,1:T(1,128)S(1)}, s32[3,1]{0,1:T(1,128)}, u32[]{:S(2)}) copy-start(s32[3,1]{0,1:T(1,128)} %constant.143) | copy-start | bytes 40
  61.1 8.6 %copy-start.10 = (f32[3,128,16]{1,2,0:T(8,128)S(1)}, f32[3,128,16]{1,2,0:T(8,128)}, u32[]{:S(2)}) copy-start(f32[3,128,16]{1,2,0:T(8,128)} %param.20) | copy-start | bytes 73732
  75.1 48.5 %copy-start.6 = (bf16[128,3072]{0,1:T(8,128)(2,1)S(1)}, bf16[128,3072]{0,1:T(8,128)(2,1)}, u32[]{:S(2)}) copy-start(bf16[128,3072]{0,1:T(8,128)(2,1)} %copy.91) | copy-start | bytes 2359300
  79.7 32.8 %collective-permute-start.5 = (bf16[128,128]{0,1:T(8,128)(2,1)S(1)}, bf16[128,128]{0,1:T(8,128)(2,1)S(1)}, u32[]{:S(2)}, u32[]{:S(2)}) collective-permute-start(bf16[128,128]{0,1:T(8,128)(2,1)S(1)} %copy.92), channel_id=1, source_target_pairs={{0,12},{4,16},{8,20},{12,24},{16,28},{20,32},{24,36},{28,40},{32,4... | collective-permute-start | bytes 98312 | tf_op jit(solution)/shard_map/ppermute | solution.py:15
  112.5 8.1 %collective-permute-start.6 = (bf16[128,128]{0,1:T(8,128)(2,1)S(1)}, bf16[128,128]{0,1:T(8,128)(2,1)S(1)}, u32[]{:S(2)}, u32[]{:S(2)}) collective-permute-start(bf16[128,128]{0,1:T(8,128)(2,1)S(1)} %copy.92), channel_id=1, source_target_pairs={{0,8},{4,12},{8,16},{12,20},{16,24},{20,28},{24,32},{28,36},{32,40... | collective-permute-start | bytes 98312 | tf_op jit(solution)/shard_map/ppermute | solution.py:15
  120.7 2.1 collective-permute-start.7
  128.1 19.6 %copy-start.16 = (pred[29]{0:T(512)(128)(4,1)S(1)}, pred[29]{0:T(512)(128)(4,1)}, u32[]{:S(2)}) copy-start(pred[29]{0:T(512)(128)(4,1)} %get-tuple-element.122) | copy-start | bytes 91
  128.1 211.2 %all-to-all-start.1 = ((bf16[32,4,64,192]{3,2,1,0:T(8,128)(2,1)}), bf16[32,4,64,192]{3,2,1,0:T(8,128)(2,1)}, u32[]{:S(2)}, u32[]{:S(2)}) async-start(bf16[32,4,64,192]{3,2,1,0:T(8,128)(2,1)} %broadcast_select_fusion), calls=%async_computation.1 | async-start | bytes 8388608 | tf_op jit(solution)/shard_map/all_to_all | solution.py:140
  229.7 5.8 %copy-start.2 = (f32[1024,2048]{1,0:T(8,128)S(1)}, f32[1024,2048]{1,0:T(8,128)}, u32[]{:S(2)}) copy-start(f32[1024,2048]{1,0:T(8,128)} %get-tuple-element.183) | copy-start | bytes 25165828 | tf_op jit(solution)/shard_map/while
  244.0 5.8 %copy-start.2 = (f32[1024,2048]{1,0:T(8,128)S(1)}, f32[1024,2048]{1,0:T(8,128)}, u32[]{:S(2)}) copy-start(f32[1024,2048]{1,0:T(8,128)} %get-tuple-element.183) | copy-start | bytes 25165828 | tf_op jit(solution)/shard_map/while
  258.3 5.8 %copy-start.2 = (f32[1024,2048]{1,0:T(8,128)S(1)}, f32[1024,2048]{1,0:T(8,128)}, u32[]{:S(2)}) copy-start(f32[1024,2048]{1,0:T(8,128)} %get-tuple-element.183) | copy-start | bytes 25165828 | tf_op jit(solution)/shard_map/while
  272.6 5.8 %copy-start.2 = (f32[1024,2048]{1,0:T(8,128)S(1)}, f32[1024,2048]{1,0:T(8,128)}, u32[]{:S(2)}) copy-start(f32[1024,2048]{1,0:T(8,128)} %get-tuple-element.183) | copy-start | bytes 25165828 | tf_op jit(solution)/shard_map/while
  286.8 5.8 %copy-start.2 = (f32[1024,2048]{1,0:T(8,128)S(1)}, f32[1024,2048]{1,0:T(8,128)}, u32[]{:S(2)}) copy-start(f32[1024,2048]{1,0:T(8,128)} %get-tuple-element.183) | copy-start | bytes 25165828 | tf_op jit(solution)/shard_map/while
  301.1 5.8 %copy-start.2 = (f32[1024,2048]{1,0:T(8,128)S(1)}, f32[1024,2048]{1,0:T(8,128)}, u32[]{:S(2)}) copy-start(f32[1024,2048]{1,0:T(8,128)} %get-tuple-element.183) | copy-start | bytes 25165828 | tf_op jit(solution)/shard_map/while
  315.4 5.8 %copy-start.2 = (f32[1024,2048]{1,0:T(8,128)S(1)}, f32[1024,2048]{1,0:T(8,128)}, u32[]{:S(2)}) copy-start(f32[1024,2048]{1,0:T(8,128)} %get-tuple-element.183) | copy-start | bytes 25165828 | tf_op jit(solution)/shard_map/while
  329.7 5.8 %copy-start.2 = (f32[1024,2048]{1,0:T(8,128)S(1)}, f32[1024,2048]{1,0:T(8,128)}, u32[]{:S(2)}) copy-start(f32[1024,2048]{1,0:T(8,128)} %get-tuple-element.183) | copy-start | bytes 25165828 | tf_op jit(solution)/shard_map/while
  349.5 7.0 %copy-start.1 = (bf16[4096,128]{1,0:T(8,128)(2,1)S(1)}, bf16[4096,128]{1,0:T(8,128)(2,1)}, u32[]{:S(2)}) copy-start(bf16[4096,128]{1,0:T(8,128)(2,1)} %param.16) | copy-start | bytes 3145732
  (8 other events, 14.2 us)
Sparse Core Ops, SparseCore 0:
  15.0 112.5 all-gather.2
  130.1 93.9 all-gather.4
where the time goes:
time: 365 us; the launch traced here: 363 us
  waiting for transfers between devices  102 us (28%)
  matrix products  82.9 us (23%)
  starting transfers between devices  65.1 us (18%)
  other arithmetic  57.9 us (16%)
  local copies, waits for them, and re-layouts  40.9 us (11%)
  between operations  14.1 us (4%)
    all_gather x1, waiting for transfers between devices, on_device(): piece_values = lax.all_gather(packed_values, 'ctx', axis=0, tiled=True)  69.5 us
    dot_general x8, matrix products, absorb(): lax.dot_general(query_rows, some_keys, (((1,), (1,)), ((), ())), preferre...  44.4 us
    reduce_sum x8, other arithmetic, absorb(): running_total = running_total * factor + jnp.sum(branch_weights, axis=1)  39.5 us
    ppermute x8, waiting for transfers between devices, passed_along(): lax.ppermute(value, axis, [(source, source + steps) for source in range(f...  32.7 us
    ppermute x8, starting transfers between devices, passed_along(): lax.ppermute(value, axis, [(source, source + steps) for source in range(f...  27.1 us
    dot_general x8, matrix products, absorb(): jnp.dot(branch_weights.astype(jnp.bfloat16), some_values, preferred_eleme...  23.5 us
    all_to_all x1, starting transfers between devices, on_device(): lax.all_to_all(sent_keys, 'ctx', split_axis=0, concat_axis=0, tiled=True)  17.3 us
    unnamed x51, local copies, waits for them, and re-layouts  15 us
  transfers between devices with their start and end apart: 13, of which 4 were waited for; matrix products, arithmetic and copies ran while one was open for 40% of the time, Pallas kernels for 0%

commit v1 on v0

--- a/solution.py
+++ b/solution.py
@@ -90,7 +90,11 @@
         jnp.zeros((row_count, value_width), jnp.float32),
     )
     piece_keys = lax.all_gather(packed_keys, "ctx", axis=0, tiled=True)
-    piece_values = lax.all_gather(packed_values, "ctx", axis=0, tiled=True)
+    size = lax.axis_size("ctx")
+    repeats = [size if d == 0 else 1 for d in range(packed_values.ndim)]
+    piece_values = lax.all_to_all(
+        jnp.tile(packed_values, repeats), "ctx", split_axis=0, concat_axis=0, tiled=True
+    )
     length = piece_keys.shape[0]
     stride = math.gcd(length, 1024)
     key_block = piece_keys.reshape(length // stride, stride, key_width)

time: 365 us -> 338 us (0.926)
  waiting for transfers between devices: 102 us -> 57.7 us
  blocking collectives: 0 us -> 20.9 us
  starting transfers between devices: 65.1 us -> 56.4 us
  local copies, waits for them, and re-layouts: 40.9 us -> 45.6 us
    all_gather x1 -> x0, waiting for transfers between devices: 69.5 us -> none  [on_device(): piece_values = lax.all_gather(packed_values, 'ctx', axis=0, tiled=True)]
    all_to_all x0 -> x1, blocking collectives: none -> 20.9 us  [on_device(): lax.all_to_all(asked_here, 'ctx', split_axis=0, concat_axis=0, tiled=True)]
    all_to_all x1, waiting for transfers between devices: 0.01 us -> 20.1 us  [on_device(): lax.all_to_all(sent_values, 'ctx', split_axis=0, concat_axis=0, tiled=True)]
    all_to_all x1, starting transfers between devices: 11.3 us -> 5.55 us  [on_device(): lax.all_to_all(jnp.tile(packed_values, repeats), 'ctx', split_axis=0, con...]
    ppermute x8, waiting for transfers between devices: 32.7 us -> 37.6 us  [passed_along(): lax.ppermute(value, axis, [(source, source + steps) for source in range(f...]
    all_to_all x1, starting transfers between devices: 9.34 us -> 4.77 us  [on_device(): lax.all_to_all(sent_values, 'ctx', split_axis=0, concat_axis=0, tiled=True)]
    unnamed x51 -> x49, local copies, waits for them, and re-layouts: 15 us -> 16.7 us
  transfers between devices with their start and end apart: 13 -> 12, of which waited for: 4 -> 4; matrix products, arithmetic and copies ran while one was open for 40% -> 45% of each run, Pallas kernels for 0% -> 0%
where the time goes in v1:
time: 338 us; the launch traced here: 335 us
  matrix products  82.1 us (24%)
  other arithmetic  58 us (17%)
  waiting for transfers between devices  57.7 us (17%)
  starting transfers between devices  56.4 us (17%)
  local copies, waits for them, and re-layouts  45.6 us (13%)
  blocking collectives  20.9 us (6%)
  between operations  14.1 us (4%)
    dot_general x8, matrix products, absorb(): lax.dot_general(query_rows, some_keys, (((1,), (1,)), ((), ())), preferre...  44.4 us
    reduce_sum x8, other arithmetic, absorb(): running_total = running_total * factor + jnp.sum(branch_weights, axis=1)  39.5 us
    ppermute x8, waiting for transfers between devices, passed_along(): lax.ppermute(value, axis, [(source, source + steps) for source in range(f...  37.6 us
    ppermute x8, starting transfers between devices, passed_along(): lax.ppermute(value, axis, [(source, source + steps) for source in range(f...  28.2 us
    dot_general x8, matrix products, absorb(): jnp.dot(branch_weights.astype(jnp.bfloat16), some_values, preferred_eleme...  23.5 us
    all_to_all x1, blocking collectives, on_device(): lax.all_to_all(asked_here, 'ctx', split_axis=0, concat_axis=0, tiled=True)  20.9 us
    all_to_all x1, waiting for transfers between devices, on_device(): lax.all_to_all(sent_values, 'ctx', split_axis=0, concat_axis=0, tiled=True)  20.1 us
    all_to_all x1, starting transfers between devices, on_device(): lax.all_to_all(sent_keys, 'ctx', split_axis=0, concat_axis=0, tiled=True)  17.9 us
  transfers between devices with their start and end apart: 12, of which 4 were waited for; matrix products, arithmetic and copies ran while one was open for 45% of the time, Pallas kernels for 0%

profile of v1, /device:TPU:24, one launch (start us, length us, event | category | flops | bytes accessed | tf_op | source)
XLA Modules:
  0.0 335.1 jit_solution(10130451531627202913)
XLA Ops:
  10.2 20.9 %all_to_all.25 = s32[32,1,4]{2,1,0:T(1,128)S(1)} all-to-all(s32[32,1,4]{2,1,0:T(1,128)S(1)} %bitcast.114), channel_id=1, replica_groups=mesh['ctx'=32,'pb'=2,'ga'=4] {'ctx'}, dimensions={0} | all-to-all | bytes 1024 | tf_op jit(solution)/shard_map/all_to_all | solution.py:135
  37.5 4.8 %all-to-all-start.3 = ((bf16[32,4,64,128]{3,2,1,0:T(8,128)(2,1)}), bf16[32,4,64,128]{3,2,1,0:T(8,128)(2,1)}, u32[]{:S(2)}, u32[]{:S(2)}) async-start(bf16[32,4,64,128]{3,2,1,0:T(8,128)(2,1)} %broadcast_select_fusion.1), calls=%async_computation.3 | async-start | bytes 4194304 | tf_op jit(solution)/shard_map/all_to_all | solution.py:145
  48.0 4.4 %collective-permute-start = (bf16[128,192]{0,1:T(8,128)(2,1)S(1)}, bf16[128,192]{0,1:T(8,128)(2,1)S(1)}, u32[]{:S(2)}, u32[]{:S(2)}) collective-permute-start(bf16[128,192]{0,1:T(8,128)(2,1)S(1)} %copy-done.8), channel_id=1, source_target_pairs={{0,16},{4,20},{8,24},{12,28},{16,32},{20,36},{24,40},{28,44},{32,4... | collective-permute-start | bytes 147464 | tf_op jit(solution)/shard_map/ppermute | solution.py:15
  53.7 4.1 %collective-permute-start.2 = (bf16[128,192]{0,1:T(8,128)(2,1)S(1)}, bf16[128,192]{0,1:T(8,128)(2,1)S(1)}, u32[]{:S(2)}, u32[]{:S(2)}) collective-permute-start(bf16[128,192]{0,1:T(8,128)(2,1)S(1)} %copy-done.8), channel_id=1, source_target_pairs={{0,8},{4,12},{8,16},{12,20},{16,24},{20,28},{24,32},{28,36},{32,40... | collective-permute-start | bytes 147464 | tf_op jit(solution)/shard_map/ppermute | solution.py:15
  57.8 4.3 %collective-permute-start.3 = (bf16[128,192]{0,1:T(8,128)(2,1)S(1)}, bf16[128,192]{0,1:T(8,128)(2,1)S(1)}, u32[]{:S(2)}, u32[]{:S(2)}) collective-permute-start(bf16[128,192]{0,1:T(8,128)(2,1)S(1)} %copy-done.8), channel_id=1, source_target_pairs={{0,4},{4,8},{8,12},{12,16},{16,20},{20,24},{24,28},{28,32},{32,36}... | collective-permute-start | bytes 147464 | tf_op jit(solution)/shard_map/ppermute | solution.py:15
  65.5 3.9 %copy.85 = bf16[4096,192]{1,0:T(8,128)(2,1)} copy(bf16[4096,192]{0,1:T(8,128)(2,1)} %param.15) | data formatting | bytes 3145728 | tf_op args[3]
  77.4 20.1 %all-to-all-done.3 = bf16[32,4,64,128]{3,2,1,0:T(8,128)(2,1)} async-done(((bf16[32,4,64,128]{3,2,1,0:T(8,128)(2,1)}), bf16[32,4,64,128]{3,2,1,0:T(8,128)(2,1)}, u32[]{:S(2)}, u32[]{:S(2)}) %all-to-all-start.3) | async-done | bytes 2097184 | tf_op jit(solution)/shard_map/all_to_all | solution.py:145
  99.3 5.6 %all-to-all-start = ((bf16[32,256,128]{2,1,0:T(8,128)(2,1)}), bf16[32,256,128]{2,1,0:T(8,128)(2,1)}, u32[]{:S(2)}, u32[]{:S(2)}) async-start(bf16[32,256,128]{2,1,0:T(8,128)(2,1)} %tile.2), calls=%async_computation | async-start | bytes 4194304 | tf_op jit(solution)/shard_map/all_to_all | solution.py:95
  105.3 4.5 %gather_fusion = bf16[128,64,192]{2,1,0:T(8,128)(2,1)} fusion(bf16[64,64,192]{2,1,0:T(8,128)(2,1)} %bitcast.102, s32[1024]{0:T(1024)} %copy-done.14), kind=kCustom, calls=%fused_computation | custom fusion | bytes 6291968 | tf_op jit(solution)/shard_map/jit(_take)/gather | solution.py:138
  109.8 4.6 %broadcast_select_fusion = bf16[32,4,64,192]{3,2,1,0:T(8,128)(2,1)} fusion(bf16[32,4,64,192]{3,2,1,0:T(8,128)(2,1)} %bitcast.103, pred[32,4]{1,0:T(8,128)(4,1)S(1)} %copy.84), kind=kLoop, calls=%fused_computation.42 | loop fusion | flops 1572864 | bytes 6291584 | tf_op jit(solution)/shard_map/jit(_take)/select_n | solution.py:138
  116.5 35.4 %collective-permute-done.5 = bf16[128,128]{0,1:T(8,128)(2,1)S(1)} collective-permute-done((bf16[128,128]{0,1:T(8,128)(2,1)S(1)}, bf16[128,128]{0,1:T(8,128)(2,1)S(1)}, u32[]{:S(2)}, u32[]{:S(2)}) %collective-permute-start.5) | collective-permute-done | bytes 32800 | tf_op jit(solution)/shard_map/ppermute | solution.py:15
  151.8 8.0 %collective-permute-start.6 = (bf16[128,128]{0,1:T(8,128)(2,1)S(1)}, bf16[128,128]{0,1:T(8,128)(2,1)S(1)}, u32[]{:S(2)}, u32[]{:S(2)}) collective-permute-start(bf16[128,128]{0,1:T(8,128)(2,1)S(1)} %copy.92), channel_id=1, source_target_pairs={{0,8},{4,12},{8,16},{12,20},{16,24},{20,28},{24,32},{28,36},{32,40... | collective-permute-start | bytes 98312 | tf_op jit(solution)/shard_map/ppermute | solution.py:15
  172.2 6.0 %copy.102 = bf16[8192,192]{1,0:T(8,128)(2,1)} copy(bf16[8192,192]{0,1:T(8,128)(2,1)} %all-gather.2.cloned.1.call-done) | data formatting | bytes 6291456
  178.1 17.9 %all-to-all-start.2 = ((bf16[32,4,64,192]{3,2,1,0:T(8,128)(2,1)}), bf16[32,4,64,192]{3,2,1,0:T(8,128)(2,1)}, u32[]{:S(2)}, u32[]{:S(2)}) async-start(bf16[32,4,64,192]{3,2,1,0:T(8,128)(2,1)} %broadcast_select_fusion), calls=%async_computation.2 | async-start | bytes 8388608 | tf_op jit(solution)/shard_map/all_to_all | solution.py:144
  196.0 114.4 %while.15 = (s32[]{:T(128)}, f32[2048]{0:T(1024)S(1)}, f32[2048]{0:T(1024)S(1)}, f32[2048,128]{1,0:T(8,128)S(1)}, bf16[8,1024,192]{2,1,0:T(8,128)(2,1)}, /*index...) while((s32[]{:T(128)}, f32[2048]{0:T(1024)S(1)}, ...), condition=%wide.region_7.8_spmd.clone, body=%wide.region_4.7_spmd.clone.sunk | while | flops 1359751168 | bytes 62522500 | solution.py:121
  196.1 5.6 %multiply_reduce_fusion.2 = (f32[2048]{0:T(1024)S(1)}, f32[1024,2048]{1,0:T(8,128)}) fusion(bf16[2048,192]{1,0:T(8,128)(2,1)S(1)} %get-tuple-element.209, bf16[8,1024,192]{2,1,0:T(8,128)(2,1)} %get-tuple-element.208, s32[]{:T(128)} %get-tuple-element.195), kind=kOutput, calls=%fused_computation.5.clone.1 | convolution fusion | flops 809498624 | bytes 9708032 | tf_op jit(solution)/shard_map/while/body/eval_jaxpr/dot_general | solution.py:107
  201.6 4.9 %fusion.72 = f32[2048]{0:T(1024)S(1)} fusion(f32[1024,2048]{1,0:T(8,128)} %get-tuple-element.183, f32[2048]{0:T(1024)S(1)} %select_maximum_fusion.2), kind=kLoop, calls=%fused_computation.7.clone.1 | loop fusion | flops 6289408 | bytes 8404992 | tf_op jit(solution)/shard_map/while/body/eval_jaxpr/reduce_sum | solution.py:115
  210.4 5.6 %multiply_reduce_fusion.2 = (f32[2048]{0:T(1024)S(1)}, f32[1024,2048]{1,0:T(8,128)}) fusion(bf16[2048,192]{1,0:T(8,128)(2,1)S(1)} %get-tuple-element.209, bf16[8,1024,192]{2,1,0:T(8,128)(2,1)} %get-tuple-element.208, s32[]{:T(128)} %get-tuple-element.195), kind=kOutput, calls=%fused_computation.5.clone.1 | convolution fusion | flops 809498624 | bytes 9708032 | tf_op jit(solution)/shard_map/while/body/eval_jaxpr/dot_general | solution.py:107
  215.9 4.9 %fusion.72 = f32[2048]{0:T(1024)S(1)} fusion(f32[1024,2048]{1,0:T(8,128)} %get-tuple-element.183, f32[2048]{0:T(1024)S(1)} %select_maximum_fusion.2), kind=kLoop, calls=%fused_computation.7.clone.1 | loop fusion | flops 6289408 | bytes 8404992 | tf_op jit(solution)/shard_map/while/body/eval_jaxpr/reduce_sum | solution.py:115
  224.7 5.6 %multiply_reduce_fusion.2 = (f32[2048]{0:T(1024)S(1)}, f32[1024,2048]{1,0:T(8,128)}) fusion(bf16[2048,192]{1,0:T(8,128)(2,1)S(1)} %get-tuple-element.209, bf16[8,1024,192]{2,1,0:T(8,128)(2,1)} %get-tuple-element.208, s32[]{:T(128)} %get-tuple-element.195), kind=kOutput, calls=%fused_computation.5.clone.1 | convolution fusion | flops 809498624 | bytes 9708032 | tf_op jit(solution)/shard_map/while/body/eval_jaxpr/dot_general | solution.py:107
  230.2 4.9 %fusion.72 = f32[2048]{0:T(1024)S(1)} fusion(f32[1024,2048]{1,0:T(8,128)} %get-tuple-element.183, f32[2048]{0:T(1024)S(1)} %select_maximum_fusion.2), kind=kLoop, calls=%fused_computation.7.clone.1 | loop fusion | flops 6289408 | bytes 8404992 | tf_op jit(solution)/shard_map/while/body/eval_jaxpr/reduce_sum | solution.py:115
  239.0 5.6 %multiply_reduce_fusion.2 = (f32[2048]{0:T(1024)S(1)}, f32[1024,2048]{1,0:T(8,128)}) fusion(bf16[2048,192]{1,0:T(8,128)(2,1)S(1)} %get-tuple-element.209, bf16[8,1024,192]{2,1,0:T(8,128)(2,1)} %get-tuple-element.208, s32[]{:T(128)} %get-tuple-element.195), kind=kOutput, calls=%fused_computation.5.clone.1 | convolution fusion | flops 809498624 | bytes 9708032 | tf_op jit(solution)/shard_map/while/body/eval_jaxpr/dot_general | solution.py:107
  244.5 4.9 %fusion.72 = f32[2048]{0:T(1024)S(1)} fusion(f32[1024,2048]{1,0:T(8,128)} %get-tuple-element.183, f32[2048]{0:T(1024)S(1)} %select_maximum_fusion.2), kind=kLoop, calls=%fused_computation.7.clone.1 | loop fusion | flops 6289408 | bytes 8404992 | tf_op jit(solution)/shard_map/while/body/eval_jaxpr/reduce_sum | solution.py:115
  253.3 5.6 %multiply_reduce_fusion.2 = (f32[2048]{0:T(1024)S(1)}, f32[1024,2048]{1,0:T(8,128)}) fusion(bf16[2048,192]{1,0:T(8,128)(2,1)S(1)} %get-tuple-element.209, bf16[8,1024,192]{2,1,0:T(8,128)(2,1)} %get-tuple-element.208, s32[]{:T(128)} %get-tuple-element.195), kind=kOutput, calls=%fused_computation.5.clone.1 | convolution fusion | flops 809498624 | bytes 9708032 | tf_op jit(solution)/shard_map/while/body/eval_jaxpr/dot_general | solution.py:107
  258.8 4.9 %fusion.72 = f32[2048]{0:T(1024)S(1)} fusion(f32[1024,2048]{1,0:T(8,128)} %get-tuple-element.183, f32[2048]{0:T(1024)S(1)} %select_maximum_fusion.2), kind=kLoop, calls=%fused_computation.7.clone.1 | loop fusion | flops 6289408 | bytes 8404992 | tf_op jit(solution)/shard_map/while/body/eval_jaxpr/reduce_sum | solution.py:115
  267.6 5.6 %multiply_reduce_fusion.2 = (f32[2048]{0:T(1024)S(1)}, f32[1024,2048]{1,0:T(8,128)}) fusion(bf16[2048,192]{1,0:T(8,128)(2,1)S(1)} %get-tuple-element.209, bf16[8,1024,192]{2,1,0:T(8,128)(2,1)} %get-tuple-element.208, s32[]{:T(128)} %get-tuple-element.195), kind=kOutput, calls=%fused_computation.5.clone.1 | convolution fusion | flops 809498624 | bytes 9708032 | tf_op jit(solution)/shard_map/while/body/eval_jaxpr/dot_general | solution.py:107
  273.1 4.9 %fusion.72 = f32[2048]{0:T(1024)S(1)} fusion(f32[1024,2048]{1,0:T(8,128)} %get-tuple-element.183, f32[2048]{0:T(1024)S(1)} %select_maximum_fusion.2), kind=kLoop, calls=%fused_computation.7.clone.1 | loop fusion | flops 6289408 | bytes 8404992 | tf_op jit(solution)/shard_map/while/body/eval_jaxpr/reduce_sum | solution.py:115
  281.9 5.6 %multiply_reduce_fusion.2 = (f32[2048]{0:T(1024)S(1)}, f32[1024,2048]{1,0:T(8,128)}) fusion(bf16[2048,192]{1,0:T(8,128)(2,1)S(1)} %get-tuple-element.209, bf16[8,1024,192]{2,1,0:T(8,128)(2,1)} %get-tuple-element.208, s32[]{:T(128)} %get-tuple-element.195), kind=kOutput, calls=%fused_computation.5.clone.1 | convolution fusion | flops 809498624 | bytes 9708032 | tf_op jit(solution)/shard_map/while/body/eval_jaxpr/dot_general | solution.py:107
  287.4 4.9 %fusion.72 = f32[2048]{0:T(1024)S(1)} fusion(f32[1024,2048]{1,0:T(8,128)} %get-tuple-element.183, f32[2048]{0:T(1024)S(1)} %select_maximum_fusion.2), kind=kLoop, calls=%fused_computation.7.clone.1 | loop fusion | flops 6289408 | bytes 8404992 | tf_op jit(solution)/shard_map/while/body/eval_jaxpr/reduce_sum | solution.py:115
  296.2 5.6 %multiply_reduce_fusion.2 = (f32[2048]{0:T(1024)S(1)}, f32[1024,2048]{1,0:T(8,128)}) fusion(bf16[2048,192]{1,0:T(8,128)(2,1)S(1)} %get-tuple-element.209, bf16[8,1024,192]{2,1,0:T(8,128)(2,1)} %get-tuple-element.208, s32[]{:T(128)} %get-tuple-element.195), kind=kOutput, calls=%fused_computation.5.clone.1 | convolution fusion | flops 809498624 | bytes 9708032 | tf_op jit(solution)/shard_map/while/body/eval_jaxpr/dot_general | solution.py:107
  301.7 4.9 %fusion.72 = f32[2048]{0:T(1024)S(1)} fusion(f32[1024,2048]{1,0:T(8,128)} %get-tuple-element.183, f32[2048]{0:T(1024)S(1)} %select_maximum_fusion.2), kind=kLoop, calls=%fused_computation.7.clone.1 | loop fusion | flops 6289408 | bytes 8404992 | tf_op jit(solution)/shard_map/while/body/eval_jaxpr/reduce_sum | solution.py:115
  321.3 4.9 %add_convert_fusion = bf16[128,16,128]{0,2,1:T(8,128)(2,1)} fusion(f32[128,16,128]{0,2,1:T(8,128)S(1)} %copy.90, f32[128,16,128]{0,2,1:T(8,128)S(1)} %copy.81, f32[640,128,16]{1,0,2:T(8,128)} %copy-done.5, f32[128,16]{0,1:T(8,128)S(1)} %get-tuple-element.133, pred[128,640]{0,1:T(8,128)(4,1)S(1)} %fusion.44, f32[128,16]{0,1:T(8,128)S(1)} %fusion.21, ...), kind=kOutput, calls=%fused_computation.54 | convolution fusion | flops 342622208 | bytes 8151040 | tf_op jit(solution)/shard_map/qhk,kv->qhv/dot_general | solution.py:220
  (177 shorter events, 87.6 us)
Async XLA Ops:
  6.5 25.6 %copy-start = (bf16[4096,128]{1,0:T(8,128)(2,1)S(1)}, bf16[4096,128]{1,0:T(8,128)(2,1)}, u32[]{:S(2)}) copy-start(bf16[4096,128]{1,0:T(8,128)(2,1)} %param.16) | copy-start | bytes 3145732
  31.9 5.6 %copy-start.14 = (s32[1024]{0:T(1024)}, s32[1024]{0:T(1024)S(1)}, u32[]{:S(2)}) copy-start(s32[1024]{0:T(1024)S(1)} %pad_clamp_fusion.1) | copy-start | bytes 12292
  34.3 8.1 %copy-start.11 = (s32[1,256]{1,0:T(1,128)S(1)}, s32[1,256]{1,0:T(1,128)}, u32[]{:S(2)}) copy-start(s32[1,256]{1,0:T(1,128)} %param.17) | copy-start | bytes 3076
  34.3 10.1 %copy-start.17 = (f32[1,32]{1,0:T(1,128)S(1)}, f32[1,32]{1,0:T(1,128)}, u32[]{:S(2)}) copy-start(f32[1,32]{1,0:T(1,128)} %param.18) | copy-start | bytes 388
  37.5 60.0 %all-to-all-start.3 = ((bf16[32,4,64,128]{3,2,1,0:T(8,128)(2,1)}), bf16[32,4,64,128]{3,2,1,0:T(8,128)(2,1)}, u32[]{:S(2)}, u32[]{:S(2)}) async-start(bf16[32,4,64,128]{3,2,1,0:T(8,128)(2,1)} %broadcast_select_fusion.1), calls=%async_computation.3 | async-start | bytes 4194304 | tf_op jit(solution)/shard_map/all_to_all | solution.py:145
  42.3 129.9 %all-gather.2.cloned.1.call-start = ((), (), s32[]{:S(2)}) async-start(), calls=%async_computation.4 | async-start | bytes 3244032 | tf_op jit(solution)/shard_map/all_gather | solution.py:92
  44.6 17.6 %copy-start.9 = (bf16[128,128]{1,0:T(8,128)(2,1)S(1)}, bf16[128,128]{1,0:T(8,128)(2,1)}, u32[]{:S(2)}) copy-start(bf16[128,128]{1,0:T(8,128)(2,1)} %param.14) | copy-start | bytes 98308
  44.6 24.8 %copy-start.3 = (bf16[128,3072]{1,0:T(8,128)(2,1)S(1)}, bf16[128,3072]{1,0:T(8,128)(2,1)}, u32[]{:S(2)}) copy-start(bf16[128,3072]{1,0:T(8,128)(2,1)} %param.12) | copy-start | bytes 2359300
  48.0 116.3 %collective-permute-start = (bf16[128,192]{0,1:T(8,128)(2,1)S(1)}, bf16[128,192]{0,1:T(8,128)(2,1)S(1)}, u32[]{:S(2)}, u32[]{:S(2)}) collective-permute-start(bf16[128,192]{0,1:T(8,128)(2,1)S(1)} %copy-done.8), channel_id=1, source_target_pairs={{0,16},{4,20},{8,24},{12,28},{16,32},{20,36},{24,40},{28,44},{32,4... | collective-permute-start | bytes 147464 | tf_op jit(solution)/shard_map/ppermute | solution.py:15
  52.4 111.9 %collective-permute-start.1 = (bf16[128,192]{0,1:T(8,128)(2,1)S(1)}, bf16[128,192]{0,1:T(8,128)(2,1)S(1)}, u32[]{:S(2)}, u32[]{:S(2)}) collective-permute-start(bf16[128,192]{0,1:T(8,128)(2,1)S(1)} %copy-done.8), channel_id=1, source_target_pairs={{0,12},{4,16},{8,20},{12,24},{16,28},{20,32},{24,36},{28,40},{32,4... | collective-permute-start | bytes 147464 | tf_op jit(solution)/shard_map/ppermute | solution.py:15
  53.7 110.6 %collective-permute-start.2 = (bf16[128,192]{0,1:T(8,128)(2,1)S(1)}, bf16[128,192]{0,1:T(8,128)(2,1)S(1)}, u32[]{:S(2)}, u32[]{:S(2)}) collective-permute-start(bf16[128,192]{0,1:T(8,128)(2,1)S(1)} %copy-done.8), channel_id=1, source_target_pairs={{0,8},{4,12},{8,16},{12,20},{16,24},{20,28},{24,32},{28,36},{32,40... | collective-permute-start | bytes 147464 | tf_op jit(solution)/shard_map/ppermute | solution.py:15
  57.8 106.5 %collective-permute-start.3 = (bf16[128,192]{0,1:T(8,128)(2,1)S(1)}, bf16[128,192]{0,1:T(8,128)(2,1)S(1)}, u32[]{:S(2)}, u32[]{:S(2)}) collective-permute-start(bf16[128,192]{0,1:T(8,128)(2,1)S(1)} %copy-done.8), channel_id=1, source_target_pairs={{0,4},{4,8},{8,12},{12,16},{16,20},{20,24},{24,28},{28,32},{32,36}... | collective-permute-start | bytes 147464 | tf_op jit(solution)/shard_map/ppermute | solution.py:15
  62.3 13.8 %copy-start.16 = (s32[2,1,13]{2,1,0:T(1,128)S(1)}, s32[2,1,13]{2,1,0:T(1,128)}, u32[]{:S(2)}) copy-start(s32[2,1,13]{2,1,0:T(1,128)} %param.19) | copy-start | bytes 316
  62.3 52.1 %collective-permute-start.4 = (bf16[128,128]{0,1:T(8,128)(2,1)S(1)}, bf16[128,128]{0,1:T(8,128)(2,1)}, u32[]{:S(2)}, u32[]{:S(2)}) collective-permute-start(bf16[128,128]{0,1:T(8,128)(2,1)S(1)} %copy.92), channel_id=1, source_target_pairs={{0,16},{4,20},{8,24},{12,28},{16,32},{20,36},{24,40},{28,44},{32,4... | collective-permute-start | bytes 98312 | tf_op jit(solution)/shard_map/ppermute | solution.py:15
  77.4 27.5 %copy-start.18 = (s32[3,1]{0,1:T(1,128)S(1)}, s32[3,1]{0,1:T(1,128)}, u32[]{:S(2)}) copy-start(s32[3,1]{0,1:T(1,128)} %constant.143) | copy-start | bytes 40
  77.4 27.6 %copy-start.10 = (f32[3,128,16]{1,2,0:T(8,128)S(1)}, f32[3,128,16]{1,2,0:T(8,128)}, u32[]{:S(2)}) copy-start(f32[3,128,16]{1,2,0:T(8,128)} %param.20) | copy-start | bytes 73732
  99.3 78.8 %all-to-all-start = ((bf16[32,256,128]{2,1,0:T(8,128)(2,1)}), bf16[32,256,128]{2,1,0:T(8,128)(2,1)}, u32[]{:S(2)}, u32[]{:S(2)}) async-start(bf16[32,256,128]{2,1,0:T(8,128)(2,1)} %tile.2), calls=%async_computation | async-start | bytes 4194304 | tf_op jit(solution)/shard_map/all_to_all | solution.py:95
  109.8 54.7 %copy-start.6 = (bf16[128,3072]{0,1:T(8,128)(2,1)S(1)}, bf16[128,3072]{0,1:T(8,128)(2,1)}, u32[]{:S(2)}) copy-start(bf16[128,3072]{0,1:T(8,128)(2,1)} %copy.91) | copy-start | bytes 2359300
  114.4 37.4 %collective-permute-start.5 = (bf16[128,128]{0,1:T(8,128)(2,1)S(1)}, bf16[128,128]{0,1:T(8,128)(2,1)S(1)}, u32[]{:S(2)}, u32[]{:S(2)}) collective-permute-start(bf16[128,128]{0,1:T(8,128)(2,1)S(1)} %copy.92), channel_id=1, source_target_pairs={{0,12},{4,16},{8,20},{12,24},{16,28},{20,32},{24,36},{28,40},{32,4... | collective-permute-start | bytes 98312 | tf_op jit(solution)/shard_map/ppermute | solution.py:15
  151.8 9.6 %collective-permute-start.6 = (bf16[128,128]{0,1:T(8,128)(2,1)S(1)}, bf16[128,128]{0,1:T(8,128)(2,1)S(1)}, u32[]{:S(2)}, u32[]{:S(2)}) collective-permute-start(bf16[128,128]{0,1:T(8,128)(2,1)S(1)} %copy.92), channel_id=1, source_target_pairs={{0,8},{4,12},{8,16},{12,20},{16,24},{20,28},{24,32},{28,36},{32,40... | collective-permute-start | bytes 98312 | tf_op jit(solution)/shard_map/ppermute | solution.py:15
  161.5 2.1 collective-permute-start.7
  165.4 5.7 %copy-start.15 = (pred[29]{0:T(512)(128)(4,1)S(1)}, pred[29]{0:T(512)(128)(4,1)}, u32[]{:S(2)}) copy-start(pred[29]{0:T(512)(128)(4,1)} %get-tuple-element.122) | copy-start | bytes 91
  178.1 133.1 %all-to-all-start.2 = ((bf16[32,4,64,192]{3,2,1,0:T(8,128)(2,1)}), bf16[32,4,64,192]{3,2,1,0:T(8,128)(2,1)}, u32[]{:S(2)}, u32[]{:S(2)}) async-start(bf16[32,4,64,192]{3,2,1,0:T(8,128)(2,1)} %broadcast_select_fusion), calls=%async_computation.2 | async-start | bytes 8388608 | tf_op jit(solution)/shard_map/all_to_all | solution.py:144
  201.6 5.8 %copy-start.2 = (f32[1024,2048]{1,0:T(8,128)S(1)}, f32[1024,2048]{1,0:T(8,128)}, u32[]{:S(2)}) copy-start(f32[1024,2048]{1,0:T(8,128)} %get-tuple-element.183) | copy-start | bytes 25165828 | tf_op jit(solution)/shard_map/while
  215.9 5.8 %copy-start.2 = (f32[1024,2048]{1,0:T(8,128)S(1)}, f32[1024,2048]{1,0:T(8,128)}, u32[]{:S(2)}) copy-start(f32[1024,2048]{1,0:T(8,128)} %get-tuple-element.183) | copy-start | bytes 25165828 | tf_op jit(solution)/shard_map/while
  230.2 5.8 %copy-start.2 = (f32[1024,2048]{1,0:T(8,128)S(1)}, f32[1024,2048]{1,0:T(8,128)}, u32[]{:S(2)}) copy-start(f32[1024,2048]{1,0:T(8,128)} %get-tuple-element.183) | copy-start | bytes 25165828 | tf_op jit(solution)/shard_map/while
  244.5 5.8 %copy-start.2 = (f32[1024,2048]{1,0:T(8,128)S(1)}, f32[1024,2048]{1,0:T(8,128)}, u32[]{:S(2)}) copy-start(f32[1024,2048]{1,0:T(8,128)} %get-tuple-element.183) | copy-start | bytes 25165828 | tf_op jit(solution)/shard_map/while
  258.8 5.8 %copy-start.2 = (f32[1024,2048]{1,0:T(8,128)S(1)}, f32[1024,2048]{1,0:T(8,128)}, u32[]{:S(2)}) copy-start(f32[1024,2048]{1,0:T(8,128)} %get-tuple-element.183) | copy-start | bytes 25165828 | tf_op jit(solution)/shard_map/while
  273.1 5.8 %copy-start.2 = (f32[1024,2048]{1,0:T(8,128)S(1)}, f32[1024,2048]{1,0:T(8,128)}, u32[]{:S(2)}) copy-start(f32[1024,2048]{1,0:T(8,128)} %get-tuple-element.183) | copy-start | bytes 25165828 | tf_op jit(solution)/shard_map/while
  287.4 5.8 %copy-start.2 = (f32[1024,2048]{1,0:T(8,128)S(1)}, f32[1024,2048]{1,0:T(8,128)}, u32[]{:S(2)}) copy-start(f32[1024,2048]{1,0:T(8,128)} %get-tuple-element.183) | copy-start | bytes 25165828 | tf_op jit(solution)/shard_map/while
  301.7 5.8 %copy-start.2 = (f32[1024,2048]{1,0:T(8,128)S(1)}, f32[1024,2048]{1,0:T(8,128)}, u32[]{:S(2)}) copy-start(f32[1024,2048]{1,0:T(8,128)} %get-tuple-element.183) | copy-start | bytes 25165828 | tf_op jit(solution)/shard_map/while
  321.2 7.0 %copy-start.1 = (bf16[4096,128]{1,0:T(8,128)(2,1)S(1)}, bf16[4096,128]{1,0:T(8,128)(2,1)}, u32[]{:S(2)}) copy-start(bf16[4096,128]{1,0:T(8,128)(2,1)} %param.16) | copy-start | bytes 3145732
  (6 other events, 12.8 us)
Sparse Core Ops, SparseCore 0:
  48.1 118.3 all-gather.1
